TPU v7x, 32 devices: a whole 2x2x4 slice. The times are simulated.
32 devices in a mesh: rep: 8 (over z, x), tp: 4 (over y, core).
Axes of the slice: x: 2, y: 2, z: 4, core: 2. Of those that a mesh axis runs over, the one named last changes fastest.
Arguments:
- q_weight: float32 [5120, 5120], P(('rep', 'tp')), may hold values from -0.078125 to 0.078125
- key_projection_weight: float32 [1024, 5120], P(('rep', 'tp')), may hold values from -0.078125 to 0.078125
- value_projection_weight: float32 [1024, 5120], P(('rep', 'tp')), may hold values from -0.078125 to 0.078125
- tokens: bfloat16 [8192, 5120], P(('rep', 'tp')), may hold values from -6 to 6
Outputs:
- combined_query_key_value: bfloat16 [7168, 5120], P('tp')
- projected: bfloat16 [8192, 7168], P('rep', 'tp')
All inputs are finite; a program needn't handle non-finite values.
Results may differ from a plain program's by a relative error of at most 0.0049.
Values may be sent and summed in bfloat16 or wider, within the bound.
A program may use at most 192 MiB of HBM per device.

v0:
```python
import functools

import jax
import jax.numpy as jnp
from jax import lax
from jax.experimental import pallas as pl
from jax.experimental.pallas import tpu as pltpu
from jax.sharding import PartitionSpec as P

MESH = pl.DeviceIdType.MESH
LEAD = 3
Y_LAG = 2
TOK_AT = 11
LATE_FIRST = 1
LATE_EVERY = 2


def gather_kernel(
    rep_size, tp_size, q_rows, kv_rows,
    shard, tok, weights, projected,
    prompts, relay, shard_buf, block_buf, result_buf, local_sem, block_sem, result_sem,
    part_send, part_recv, z_send, z_recv, y_send, y_recv, x_send, x_recv, tok_send, tok_recv,
):
    planes = tp_size
    columns = rep_size // planes
    half = tp_size // 2
    r, t = lax.axis_index("rep"), lax.axis_index("tp")
    plane, column = r // columns, r % columns
    side, core = t // 2, t % 2
    other = (t + half) % tp_size
    partner = t + 1 - 2 * core
    q_chunks = q_rows // kv_rows
    pieces = q_chunks + 2
    count = 2 * pieces
    shards_in_plane = tp_size * columns
    ranks = (t, other)
    order = (q_chunks, q_chunks + 1) + tuple(range(q_chunks))

    def row_of(index, m):
        if m < q_chunks:
            return pl.multiple_of(index * q_rows + m * kv_rows, 8)
        base = shards_in_plane * (q_rows + (m - q_chunks) * kv_rows)
        return pl.multiple_of(base + index * kv_rows, 8)

    def in_weights(at_side, n):
        of_core = core if n < pieces else 1 - core
        return weights.at[pl.ds(row_of(column * tp_size + at_side * 2 + of_core, order[n % pieces]), kv_rows)]

    def in_relay(n):
        return relay.at[pl.ds(n * kv_rows, kv_rows)]

    def in_shard(n):
        return shard.at[pl.ds(order[n] * kv_rows, kv_rows)]

    def place(slot, n):
        return in_weights(side, n) if slot == 0 else in_relay(n)

    def remote(src, dst, send, recv, to_rep, to_tp):
        return pltpu.make_async_remote_copy(
            src_ref=src, dst_ref=dst, send_sem=send, recv_sem=recv,
            device_id=(to_rep, to_tp), device_id_type=MESH,
        )

    def ups(slot):
        k = ranks[slot]
        return (plane >= k) & (plane < planes - 1), (plane <= k) & (plane > 0)

    def x_sends(n, src, dst, which):
        kind = 0 if n % pieces < 2 else 1 + which
        for d in range(1, columns):
            to = plane * columns + (column + d) % columns
            remote(src, dst, x_send.at[d - 1], x_recv.at[d - 1, kind], to, t).start()

    def forward(slot, n, src, from_source=False):
        up, down = ups(slot)
        if from_source:
            up, down = up & (plane != planes - 2), down & (plane != 1)
        dst = place(slot, n)

        @pl.when(up)
        def _():
            remote(src, dst, z_send.at[slot, 0], z_recv.at[slot, n], r + columns, t).start()

        @pl.when(down)
        def _():
            remote(src, dst, z_send.at[slot, 1], z_recv.at[slot, n], r - columns, t).start()

        if slot == 0:
            x_sends(n, src, dst, 0)
        else:
            remote(src, in_weights(side, n), y_send.at[0], y_recv.at[n], r, other).start()

    def recv_wait(dst, sem):
        remote(dst, dst, x_send.at[0], sem, r, partner).wait_recv()

    def send_wait(src, sem):
        remote(src, src, sem, x_recv.at[0, 0], r, partner).wait_send()

    def source_step(slot, n):
        @pl.when(plane == ranks[slot])
        def _():
            if n < pieces:
                forward(slot, n, in_shard(n), True)
            else:
                recv_wait(place(slot, n), part_recv.at[n - pieces])
                forward(slot, n, place(slot, n), True)

    def late_step(slot, n):
        up, down = ups(slot)
        src, dst = in_shard(n) if n < pieces else place(slot, n), place(slot, n)

        @pl.when((plane == ranks[slot]) & up & (plane == planes - 2))
        def _():
            remote(src, dst, z_send.at[slot, 0], z_recv.at[slot, n], r + columns, t).start()

        @pl.when((plane == ranks[slot]) & down & (plane == 1))
        def _():
            remote(src, dst, z_send.at[slot, 1], z_recv.at[slot, n], r - columns, t).start()

    def relay_step(slot, n):
        @pl.when(plane != ranks[slot])
        def _():
            recv_wait(place(slot, n), z_recv.at[slot, n])
            forward(slot, n, place(slot, n))

    def y_step(n):
        block = in_weights(1 - side, n)
        recv_wait(block, y_recv.at[n])
        x_sends(n, block, block, 1)

    rows = tok.shape[0]

    def prompt_rows(rank):
        return prompts.at[pl.ds(pl.multiple_of(rank * rows, 8), rows)]

    handler = core == plane % 2
    load_shard = pltpu.make_async_copy(shard, shard_buf, local_sem.at[0])
    load_tok = pltpu.make_async_copy(tok, prompt_rows(t), local_sem.at[1])
    load_shard.start()
    load_tok.start()

    @pl.when(jnp.logical_not(handler))
    def _():
        for m in range(pieces):
            @pl.when(side == plane // 2)
            def _():
                dst = weights.at[pl.ds(row_of(column * tp_size + t, order[m]), kv_rows)]
                remote(in_shard(m), dst, part_send.at[0], part_recv.at[m], r, partner).start()

            @pl.when(side != plane // 2)
            def _():
                remote(in_shard(m), in_relay(pieces + m), part_send.at[0], part_recv.at[m], r, partner).start()

    remote(tok, prompt_rows(t), tok_send.at[1], tok_recv.at[1], r, partner).start()

    for n in range(LEAD):
        source_step(0, n)
        source_step(1, n)

    load_shard.wait()
    load_tok.wait()

    def store_shard(m):
        dst = weights.at[pl.ds(row_of(column * tp_size + t, m), kv_rows)]
        return pltpu.make_async_copy(shard_buf.at[pl.ds(m * kv_rows, kv_rows)], dst, local_sem.at[2 + m])

    @pl.when(plane == t)
    def _():
        for m in range(pieces):
            store_shard(m).start()

    late = 0
    for n in range(LATE_FIRST):
        late_step(0, n)
        late_step(1, n)
        late += 1
    for n in range(count):
        if n % LATE_EVERY == LATE_EVERY - 1 and late < count:
            late_step(0, late)
            late_step(1, late)
            late += 1
        if n + LEAD < count:
            source_step(0, n + LEAD)
            source_step(1, n + LEAD)
        relay_step(0, n)
        relay_step(1, n)
        if n == TOK_AT:
            remote(tok, prompt_rows(t), tok_send.at[0], tok_recv.at[0], r, other).start()
        if n >= Y_LAG:
            y_step(n - Y_LAG)
    for n in range(late, count):
        late_step(0, n)
        late_step(1, n)
    for n in range(count - Y_LAG, count):
        y_step(n)
    recv_wait(prompt_rows(other), tok_recv.at[0])
    remote(prompt_rows(other), prompt_rows(other), tok_send.at[2], tok_recv.at[2], r, partner).start()

    recv_wait(prompt_rows(partner), tok_recv.at[1])
    recv_wait(prompt_rows((partner + half) % tp_size), tok_recv.at[2])

    @pl.when(plane == t)
    def _():
        for m in range(pieces):
            store_shard(m).wait()

    block = block_buf.shape[1]
    token_tile = min(256, prompts.shape[0])
    quarter = count * kv_rows
    own = tp_size * q_rows
    firsts = [-(-(c * own) // block) for c in range(columns)]
    early = min((c + 1) * own // block - firsts[c] for c in range(columns))
    early = max(early, 0)
    q_blocks = columns * own // block
    first = (column * own + block - 1) // block

    def load_block(index, at):
        src = weights.at[pl.ds(pl.multiple_of(index * block, block), block)]
        return pltpu.make_async_copy(src, block_buf.at[at], block_sem.at[at])

    def store_block(index, at):
        dst = projected.at[:, pl.ds(pl.multiple_of(index * block, block), block)]
        return pltpu.make_async_copy(result_buf.at[at], dst, result_sem.at[at])

    here = [first + i for i in range(early)] + [q_blocks, q_blocks + 1]
    left = q_blocks - early
    places = [jnp.where(side == 0, i, left - 1 - i) for i in range(left)]
    last = [jnp.where(i >= first, i + early, i) for i in places]
    alone = True
    for c in range(columns):
        for s in range(2):
            i = s * (left - 1)
            low = (i + early if i >= firsts[c] else i) * block
            for part in range(low // (2 * q_rows), (low + block - 1) // (2 * q_rows) + 1):
                alone = alone and (part // 2 == c or part % 2 == s)
    blocks = here + last

    def multiply(i):
        at = i % 2
        load_block(blocks[i], at).wait()
        if i >= 2:
            store_block(blocks[i - 2], at).wait()

        @pl.loop(0, prompts.shape[0] // token_tile)
        def _(tile):
            at_rows = pl.ds(pl.multiple_of(tile * token_tile, token_tile), token_tile)
            result_buf[at, at_rows, :] = lax.dot_general(
                prompts[at_rows, :], block_buf[at], (((1,), (1,)), ((), ())),
                preferred_element_type=jnp.float32,
            ).astype(result_buf.dtype)

        store_block(blocks[i], at).start()

    kv_part = 2 * 2 * 2 * kv_rows
    if early:
        load_block(blocks[0], 0).start()
    for d in range(1, columns):
        recv_wait(weights.at[pl.ds(0, kv_part)], x_recv.at[d - 1, 0])
    if not early:
        load_block(blocks[0], 0).start()
    for i in range(len(here)):
        if i + 1 < len(here):
            load_block(blocks[i + 1], (i + 1) % 2).start()
        multiply(i)
    done = len(here)
    for which in (1, 2):
        for d in range(1, columns):
            recv_wait(weights.at[pl.ds(0, quarter - kv_part // 2)], x_recv.at[d - 1, which])
        stop = len(blocks) if which == 2 else done + int(alone)
        for i in range(done, stop):
            if i == done:
                load_block(blocks[i], i % 2).start()
            if i + 1 < stop:
                load_block(blocks[i + 1], (i + 1) % 2).start()
            multiply(i)
        done = stop
    for i in range(len(blocks) - 2, len(blocks)):
        store_block(blocks[i], i % 2).wait()

    for d in range(1, columns):
        send_wait(weights.at[pl.ds(0, 2 * quarter)], x_send.at[d - 1])
    send_wait(relay, y_send.at[0])
    for slot in range(2):
        for way, go in enumerate(ups(slot)):
            @pl.when(go)
            def _():
                send_wait(relay, z_send.at[slot, way])

    @pl.when(jnp.logical_not(handler))
    def _():
        send_wait(shard, part_send.at[0])

    for i in range(3):
        send_wait(tok, tok_send.at[i])


def gather(shard, tok, q_rows, kv_rows):
    rep_size, tp_size = lax.axis_size("rep"), lax.axis_size("tp")
    columns = rep_size // tp_size
    width = shard.shape[1]
    pieces = q_rows // kv_rows + 2
    count = 2 * pieces
    hbm = pl.BlockSpec(memory_space=pltpu.HBM)
    dma = pltpu.SemaphoreType.DMA
    block = columns * tp_size * kv_rows
    tokens = tp_size * tok.shape[0]
    total = rep_size * shard.shape[0]
    return pl.pallas_call(
        functools.partial(gather_kernel, rep_size, tp_size, q_rows, kv_rows),
        out_shape=(
            jax.ShapeDtypeStruct((total, width), shard.dtype),
            jax.ShapeDtypeStruct((tokens, total), tok.dtype),
        ),
        in_specs=[hbm, hbm],
        out_specs=(hbm, hbm),
        scratch_shapes=[
            pltpu.VMEM((tokens, width), tok.dtype),
            pltpu.VMEM((count * kv_rows, width), shard.dtype),
            pltpu.VMEM(shard.shape, shard.dtype),
            pltpu.VMEM((2, block, width), shard.dtype),
            pltpu.VMEM((2, tokens, block), tok.dtype),
            dma((2 + pieces,)), dma((2,)), dma((2,)),
            dma((1,)), dma((pieces,)),
            dma((2, 2)), dma((2, count)),
            dma((1,)), dma((count,)),
            dma((columns - 1,)), dma((columns - 1, 3)),
            dma((3,)), dma((3,)),
        ],
        compiler_params=pltpu.CompilerParams(has_side_effects=True, vmem_limit_bytes=26 * 2**20),
    )(shard, tok)


def shards(q_weight, key_projection_weight, value_projection_weight, tokens):
    shard = jnp.concatenate(
        [q_weight, key_projection_weight, value_projection_weight], 0
    ).astype(jnp.bfloat16)
    return gather(shard, tokens, q_weight.shape[0], key_projection_weight.shape[0])


def solution(mesh):
    spec = P(("rep", "tp"), None)
    return jax.shard_map(
        shards, mesh=mesh, in_specs=(spec,) * 4, out_specs=(P("tp", None), P("rep", "tp")), check_vma=False
    )
```

profile of v0, /device:TPU:24, one launch (start us, length us, event | category | flops | bytes accessed | tf_op | source)
XLA Modules:
  0.0 243.9 jit_solution(8338468079573788930)
XLA Ops:
  0.6 1.1 convert.10
  1.8 1.1 convert.11
  2.9 0.0 copy-start
  2.9 2.3 convert.9
  5.2 0.1 pad_maximum_fusion.shard
  5.3 0.3 copy-done
  5.6 229.8 %shard_map.59 = (bf16[1792,5120]{1,0:T(8,128)(2,1)S(1)}, bf16[1024,1792]{1,0:T(8,128)(2,1)S(1)}) custom-call(bf16[224,5120]{1,0:T(8,128)(2,1)S(1)} %pad_maximum_fusion.shard, bf16[256,5120]{1,0:T(8,128)(2,1)S(1)} %copy-done), custom_call_target="tpu_custom_call" | custom-call | tf_op jit(solution)/shard_map/pallas_call | solution.py:308
  235.4 6.7 %copy.8 = bf16[1792,5120]{1,0:T(8,128)(2,1)} copy(bf16[1792,5120]{1,0:T(8,128)(2,1)S(1)} %get-tuple-element.4) | data formatting | bytes 36700160
  242.1 1.8 copy.9
Async XLA Ops:
  2.9 2.7 %copy-start = (bf16[256,5120]{1,0:T(8,128)(2,1)S(1)}, bf16[256,5120]{1,0:T(8,128)(2,1)}, u32[]{:S(2)}) copy-start(bf16[256,5120]{1,0:T(8,128)(2,1)} %tok.1) | copy-start | bytes 7864324
where the time goes:
time: 247 us; the launch traced here: 244 us
  Pallas kernels  230 us (93%)
  local copies, waits for them, and re-layouts  8.79 us (4%)
  other arithmetic  4.68 us (2%)
    pallas_call x1, Pallas kernels, gather(): pl.pallas_call(functools.partial(gather_kernel, rep_size, tp_size, q_rows...  230 us
    unnamed x4, local copies, waits for them, and re-layouts  8.79 us

commit v1 on v0

v1 whole, which is shorter than its diff:
```python
import functools

import jax
import jax.numpy as jnp
from jax import lax
from jax.experimental import pallas as pl
from jax.experimental.pallas import tpu as pltpu
from jax.sharding import PartitionSpec as P

MESH = pl.DeviceIdType.MESH
LEAD = 4
Y_LAG = 3
LATE_FIRST = (4, 2)
LATE_RATE = (6, 5)
TOK_FIRST = 2
TOK_AT = 8
TOK_RATE = 2
TOK_CHUNKS = 8
TWIN_AT = 18
TWIN_RATE = 4
FAR_AT = 24
MEET_AT = 24
FIRST_AT = (99, 99)
TWICE = (17, 28)
TILE = 256
VMEM = 16


def order_of(columns, tp_size, q_rows, kv_rows, column, side):
    block = columns * tp_size * kv_rows
    own = tp_size * q_rows
    firsts = [-(-(c * own) // block) for c in range(columns)]
    early = max(min((c + 1) * own // block - firsts[c] for c in range(columns)), 0)
    q_blocks = columns * own // block
    first = (column * own + block - 1) // block
    left = q_blocks - early
    places = [jnp.where(side == 0, left - 1 - i, i) for i in range(left)]
    last = [jnp.where(i >= first, i + early, i) for i in places]
    alone = left > 1
    for c in range(columns):
        for s in range(2):
            i = 0 if s else left - 1
            low = (i + early if i >= firsts[c] else i) * block
            for part in range(low // (2 * q_rows), (low + block - 1) // (2 * q_rows) + 1):
                alone = alone and (part // 2 == c or part % 2 != s)
    here = [q_blocks, q_blocks + 1] + [first + i for i in range(early)]
    return here + last, len(here), int(alone)


def multiply(index, prompts, weights, result, at, block):
    tile = min(TILE, prompts.shape[0])
    rows = pl.ds(pl.multiple_of(index * block, block), block)
    cols = rows if at is None else pl.ds(at * block, block)

    @pl.loop(0, prompts.shape[0] // tile)
    def _(i):
        at_rows = pl.ds(pl.multiple_of(i * tile, tile), tile)
        result[at_rows, cols] = lax.dot_general(
            prompts[at_rows, :], weights[rows, :], (((1,), (1,)), ((), ())),
            preferred_element_type=jnp.float32,
        ).astype(result.dtype)


def finish_kernel(
    columns, tp_size, q_rows, kv_rows,
    weights, prompts, partial, combined, projected, result, weight_sem, partial_sem, result_sem,
):
    r, t = lax.axis_index("rep"), lax.axis_index("tp")
    block = columns * tp_size * kv_rows
    blocks, soon, late_block = order_of(columns, tp_size, q_rows, kv_rows, r % columns, t // 2)
    done = soon + late_block
    stores = []
    for i in range(weights.shape[0] // block):
        at = pl.ds(i * block, block)
        stores.append(pltpu.make_async_copy(weights.at[at], combined.at[at], weight_sem.at[i]))
    for i in range(done):
        at = pl.ds(pl.multiple_of(blocks[i] * block, block), block)
        stores.append(pltpu.make_async_copy(partial.at[:, at], projected.at[:, at], partial_sem.at[i]))
    for store in stores:
        store.start()
    for i in range(done, len(blocks)):
        multiply(blocks[i], prompts, weights, result, i - done, block)
        at = pl.ds(pl.multiple_of(blocks[i] * block, block), block)
        store = pltpu.make_async_copy(result.at[:, pl.ds((i - done) * block, block)], projected.at[:, at], result_sem.at[i - done])
        store.start()
        stores.append(store)
    for store in stores:
        store.wait()


def gather_kernel(
    rep_size, tp_size, q_rows, kv_rows, piece, twice,
    q_weight, k_weight, v_weight, tok, weights, prompts, projected,
    relay, shard, wide, load_sem, local_sem,
    part_send, part_recv, z_send, z_recv, y_send, y_recv, x_send, x_recv, tok_send, tok_recv,
    pair_recv, twin_send, twin_recv,
):
    planes = tp_size
    columns = rep_size // planes
    half = tp_size // 2
    r, t = lax.axis_index("rep"), lax.axis_index("tp")
    plane, column = r // columns, r % columns
    side, core = t // 2, t % 2
    other = (t + half) % tp_size
    partner = t + 1 - 2 * core
    split = kv_rows // piece
    q_pieces = q_rows // piece
    pieces = q_pieces + 2 * split
    count = 2 * pieces
    small = 4 * split
    shards_in_plane = tp_size * columns
    ranks = (t, other)
    sequence = [(True, m) for m in range(2 * split)] + [(False, m) for m in range(2 * split)]
    for m in range(2 * split, pieces):
        sequence += [(True, m), (False, m)]

    def shard_row(m):
        return q_rows + m * piece if m < 2 * split else (m - 2 * split) * piece

    def row_of(index, m):
        if m >= 2 * split:
            return pl.multiple_of(index * q_rows + (m - 2 * split) * piece, 8)
        base = shards_in_plane * (q_rows + (m // split) * kv_rows) + (m % split) * piece
        return pl.multiple_of(base + index * kv_rows, 8)

    def in_weights(at_column, at_side, n):
        own, m = sequence[n]
        of_core = core if own else 1 - core
        return weights.at[pl.ds(row_of(at_column * tp_size + at_side * 2 + of_core, m), piece)]

    def in_relay(n):
        return relay.at[pl.ds(n * piece, piece)]

    def in_shard(m):
        return shard.at[pl.ds(shard_row(m), piece)]

    def place(slot, n):
        return in_weights(column, side, n) if slot == 0 else in_relay(n)

    def twin_place(d, n):
        return in_weights((column - d) % columns, side, n)

    def remote(src, dst, send, recv, to_rep, to_tp):
        return pltpu.make_async_remote_copy(
            src_ref=src, dst_ref=dst, send_sem=send, recv_sem=recv,
            device_id=(to_rep, to_tp), device_id_type=MESH,
        )

    def inner(k):
        return (k > 0) & (k < planes - 1)

    def reached(k, at):
        return (at != k) & (inner(k) | (at == k + 1) | (at == k - 1))

    def is_twice(n):
        return n >= count - twice

    def ups(slot):
        k = ranks[slot]
        return (plane >= k) & (plane < planes - 1), (plane <= k) & (plane > 0)

    def held_back(slot):
        k = ranks[slot]
        return (plane == k) & (k == planes - 2), (plane == k) & (k == 1)

    def late_sink(slot):
        k = ranks[slot]
        return ((plane == planes - 1) & (k == planes - 2)) | ((plane == 0) & (k == 1))

    def x_sends(n, src, dst, sem_of):
        for d in range(1, columns):
            to = plane * columns + (column + d) % columns
            remote(src, dst, x_send.at[d - 1], sem_of(d - 1), to, t).start()

    def forward(slot, n, src, source=False):
        up, down = ups(slot)
        if source:
            late_up, late_down = held_back(slot)
            up, down = up & jnp.logical_not(late_up), down & jnp.logical_not(late_down)
        dst = place(slot, n)

        @pl.when(up)
        def _():
            remote(src, dst, z_send.at[slot, 0], z_recv.at[slot, n], r + columns, t).start()

        @pl.when(down)
        def _():
            remote(src, dst, z_send.at[slot, 1], z_recv.at[slot, n], r - columns, t).start()

        if slot == 1:
            remote(src, in_weights(column, side, n), y_send.at[0], y_recv.at[n], r, other).start()
        elif not is_twice(n):
            x_sends(n, src, dst, lambda d: x_recv.at[d, 0 if n < small else 1])
        elif source:
            x_sends(n, src, dst, lambda d: pair_recv.at[d, n - (count - twice)])
        else:
            @pl.when(jnp.logical_not(reached(t, plane)))
            def _():
                x_sends(n, src, dst, lambda d: x_recv.at[d, 3])

    def span(n):
        return weights.at[pl.ds(0, n * piece)]

    def recv_wait(dst, sem):
        remote(dst, dst, x_send.at[0], sem, r, partner).wait_recv()

    def send_wait(src, sem):
        remote(src, src, sem, x_recv.at[0, 0], r, partner).wait_send()

    def at_source(slot, n):
        own, m = sequence[n]
        return in_shard(m) if own else place(slot, n)

    taken = [0, 0]

    def take(slot, n):
        while taken[slot] <= n:
            own, m = sequence[taken[slot]]
            if not own:
                @pl.when(plane == ranks[slot])
                def _():
                    recv_wait(place(slot, taken[slot]), part_recv.at[m])
            taken[slot] += 1

    def source_step(slot, n):
        take(slot, n)

        @pl.when(plane == ranks[slot])
        def _():
            forward(slot, n, at_source(slot, n), True)

    def late_step(slot, n):
        take(slot, n)
        late_up, late_down = held_back(slot)
        src, dst = at_source(slot, n), place(slot, n)

        @pl.when(late_up)
        def _():
            remote(src, dst, z_send.at[slot, 0], z_recv.at[slot, n], r + columns, t).start()

        @pl.when(late_down)
        def _():
            remote(src, dst, z_send.at[slot, 1], z_recv.at[slot, n], r - columns, t).start()

    def relay_step(slot, n, late):
        sink = late_sink(slot)

        @pl.when((plane != ranks[slot]) & (sink if late else jnp.logical_not(sink)))
        def _():
            recv_wait(place(slot, n), z_recv.at[slot, n])
            forward(slot, n, place(slot, n))

    def y_step(n, late):
        sink = late_sink(0)

        @pl.when(sink if late else jnp.logical_not(sink))
        def _():
            block = in_weights(column, 1 - side, n)
            recv_wait(block, y_recv.at[n])
            x_sends(n, block, block, lambda d: x_recv.at[d, 0 if n < small else 2])

    goes_up = (plane >= t) & (plane < planes - 1) & reached(t, plane + 1)
    goes_down = (plane <= t) & (plane > 0) & reached(t, plane - 1)
    goes = goes_up | goes_down

    def twin_step(d, n, source):
        src = twin_place(d, n)
        at = n - (count - twice)
        here = plane == t if source else (plane != t) & goes

        @pl.when(here)
        def _():
            recv_wait(src, pair_recv.at[d - 1, at] if source else twin_recv.at[d - 1, at])

        @pl.when(here & goes_up)
        def _():
            remote(src, src, twin_send.at[0], twin_recv.at[d - 1, at], r + columns, t).start()

        @pl.when(here & goes_down)
        def _():
            remote(src, src, twin_send.at[1], twin_recv.at[d - 1, at], r - columns, t).start()

    def twin_sink(d, n):
        @pl.when(reached(t, plane) & jnp.logical_not(goes))
        def _():
            recv_wait(twin_place(d, n), twin_recv.at[d - 1, n - (count - twice)])

    handler = core == plane % 2
    rows = tok.shape[0]
    chunk = rows // TOK_CHUNKS

    def prompt_rows(rank):
        return prompts.at[pl.ds(pl.multiple_of(rank * rows, 8), rows)]

    def prompt_chunk(rank, i):
        return prompts.at[pl.ds(pl.multiple_of(rank * rows + i * chunk, 8), chunk)]

    barrier = pltpu.get_barrier_semaphore()

    def greet(to_rep, to_tp):
        pl.semaphore_signal(barrier, inc=1, device_id=(to_rep, to_tp), device_id_type=MESH)

    @pl.when(plane < planes - 1)
    def _():
        greet(r + columns, t)

    @pl.when(plane > 0)
    def _():
        greet(r - columns, t)

    for d in range(1, columns):
        greet(plane * columns + (column + d) % columns, t)
    greet(r, other)
    greet(r, partner)

    loads = [
        pltpu.make_async_copy(k_weight, wide.at[pl.ds(q_rows, kv_rows)], load_sem.at[0]),
        pltpu.make_async_copy(v_weight, wide.at[pl.ds(q_rows + kv_rows, kv_rows)], load_sem.at[1]),
        pltpu.make_async_copy(q_weight, wide.at[pl.ds(0, q_rows)], load_sem.at[2]),
    ]
    load_tok = pltpu.make_async_copy(tok, prompt_rows(t), local_sem.at[0])
    for load in loads:
        load.start()
    load_tok.start()

    def cast(m):
        at = pl.ds(shard_row(m), piece)
        value = wide[at, :].astype(shard.dtype)
        shard[at, :] = value

        @pl.when(plane == t)
        def _():
            weights[pl.ds(row_of(column * tp_size + t, m), piece), :] = value

    def part(m):
        @pl.when(jnp.logical_not(handler))
        def _():
            @pl.when(side == plane // 2)
            def _():
                dst = weights.at[pl.ds(row_of(column * tp_size + t, m), piece)]
                remote(in_shard(m), dst, part_send.at[0], part_recv.at[m], r, partner).start()

            @pl.when(side != plane // 2)
            def _():
                remote(in_shard(m), in_relay(sequence.index((False, m))), part_send.at[0], part_recv.at[m], r, partner).start()

    loads[0].wait()
    loads[1].wait()
    for m in range(2 * split):
        cast(m)
    neighbours = columns + 1 + jnp.where(inner(plane), 2, 1)
    pl.semaphore_wait(barrier, neighbours)
    for m in range(2 * split):
        part(m)
    lead = min(LEAD, 2 * split)
    for n in range(lead):
        source_step(0, n)
        source_step(1, n)
    loads[2].wait()
    for m in range(2 * split, pieces):
        cast(m)
    for m in range(2 * split, pieces):
        part(m)
    for n in range(lead, LEAD):
        source_step(0, n)
        source_step(1, n)
    load_tok.wait()
    remote(tok, prompt_rows(t), tok_send.at[1], tok_recv.at[1], r, partner).start()

    late, sunk, late_y, sent, twins, far = [0, 0], [0, 0], 0, 0, 0, 0
    pairs = [(d, n) for n in range(count - twice, count) for d in range(1, columns)]
    block = shards_in_plane * kv_rows
    blocks, soon, late_block = order_of(columns, tp_size, q_rows, kv_rows, column, side)

    def late_to(slot, stop):
        while late[slot] < min(stop, count):
            late_step(slot, late[slot])
            late[slot] += 1

    def sink_to(slot, stop):
        while sunk[slot] < min(stop, count):
            relay_step(slot, sunk[slot], True)
            sunk[slot] += 1

    def late_y_to(stop):
        nonlocal late_y
        while late_y < min(stop, count):
            y_step(late_y, True)
            late_y += 1

    def send_tokens(stop):
        nonlocal sent
        while sent < min(stop, TOK_CHUNKS):
            at = pl.ds(sent * chunk, chunk)
            remote(tok.at[at], prompt_chunk(t, sent), tok_send.at[0], tok_recv.at[0], r, other).start()
            sent += 1

    def twins_to(stop):
        nonlocal twins
        while twins < min(stop, len(pairs)):
            twin_step(*pairs[twins], True)
            twins += 1

    def far_to(stop):
        nonlocal far
        while far < min(stop, len(pairs)):
            twin_step(*pairs[far], False)
            far += 1

    def meet():
        recv_wait(prompt_rows(other), tok_recv.at[0])
        remote(prompt_rows(other), prompt_rows(other), tok_send.at[2], tok_recv.at[2], r, partner).start()

    def begin():
        recv_wait(prompt_rows(partner), tok_recv.at[1])
        recv_wait(prompt_rows((partner + half) % tp_size), tok_recv.at[2])
        for d in range(1, columns):
            recv_wait(span(2 * small), x_recv.at[d - 1, 0])

    send_tokens(TOK_FIRST)
    for slot in range(2):
        late_to(slot, LATE_FIRST[slot])
    for n in range(count):
        for slot in range(2):
            late_to(slot, LATE_FIRST[slot] + (n + 1) * LATE_RATE[slot] // 4)
        if n + LEAD < count:
            source_step(0, n + LEAD)
            source_step(1, n + LEAD)
        relay_step(0, n, False)
        relay_step(1, n, False)
        for slot in range(2):
            sink_to(slot, (n + 1) * LATE_RATE[slot] // 4)
        if n >= TOK_AT:
            send_tokens(TOK_FIRST + (n - TOK_AT) * TOK_RATE // 4 + 1)
        if n >= Y_LAG:
            y_step(n - Y_LAG, False)
        late_y_to((n + 1) * min(LATE_RATE) // 4 - Y_LAG)
        if twice and n >= TWIN_AT:
            twins_to((n - TWIN_AT) * TWIN_RATE // 4 + 1)
        if twice and n >= FAR_AT:
            far_to((n - FAR_AT) * TWIN_RATE // 4 + 1)
        if n == MEET_AT:
            meet()
        for i in range(2):
            if n == FIRST_AT[i]:
                if i == 0:
                    begin()
                multiply(blocks[i], prompts, weights, projected, None, block)
    for slot in range(2):
        late_to(slot, count)
    for n in range(count - Y_LAG, count):
        y_step(n, False)
    early = [i for i in range(2) if FIRST_AT[i] < count]
    if MEET_AT >= count:
        meet()
    if not early:
        begin()
    rest = [i for i in range(soon) if i not in early]
    twins_to(len(pairs))
    before = [i for i in rest if i < 2]
    after = [i for i in rest if i >= 2]
    steps = max(count - min(sunk), 1)
    for k in range(steps):
        for slot in range(2):
            sink_to(slot, max(sunk[slot], min(sunk) + 1) if k < steps - 1 else count)
        late_y_to(min(sunk) - Y_LAG)
        far_to(len(pairs) * (k + 1) // steps)
        if before and (k + 1) % max(steps // (len(before) + 1), 1) == 0:
            multiply(blocks[before.pop(0)], prompts, weights, projected, None, block)
    late_y_to(count)
    far_to(len(pairs))
    for i in before + after:
        multiply(blocks[i], prompts, weights, projected, None, block)
    for d in range(1, columns):
        recv_wait(span(count - small), x_recv.at[d - 1, 2])
    if late_block:
        multiply(blocks[soon], prompts, weights, projected, None, block)
    for d, n in pairs:
        twin_sink(d, n)
    for d in range(1, columns):
        recv_wait(span(count - twice - small), x_recv.at[d - 1, 1])
        if twice:
            @pl.when((plane != t) & jnp.logical_not(reached(t, plane)))
            def _():
                recv_wait(span(twice), x_recv.at[d - 1, 3])

    for d in range(1, columns):
        send_wait(span(2 * count - twice), x_send.at[d - 1])
        if twice:
            @pl.when(jnp.logical_not(reached(t, plane)))
            def _():
                send_wait(span(twice), x_send.at[d - 1])
    send_wait(relay, y_send.at[0])
    for slot in range(2):
        for way, go in enumerate(ups(slot)):
            @pl.when(go)
            def _():
                send_wait(relay, z_send.at[slot, way])
    if twice:
        @pl.when(goes_up)
        def _():
            send_wait(span(twice * (columns - 1)), twin_send.at[0])

        @pl.when(goes_down)
        def _():
            send_wait(span(twice * (columns - 1)), twin_send.at[1])

    @pl.when(jnp.logical_not(handler))
    def _():
        send_wait(shard, part_send.at[0])

    for i in range(3):
        send_wait(tok, tok_send.at[i])


def shards(q_weight, key_projection_weight, value_projection_weight, tokens):
    rep_size, tp_size = lax.axis_size("rep"), lax.axis_size("tp")
    columns = rep_size // tp_size
    q_rows, width = q_weight.shape
    kv_rows = key_projection_weight.shape[0]
    piece = kv_rows // 2 if kv_rows % 32 == 0 else kv_rows
    pieces = (q_rows + 2 * kv_rows) // piece
    count = 2 * pieces
    twice = count * TWICE[0] // TWICE[1] if columns == 2 else 0
    hbm = pl.BlockSpec(memory_space=pltpu.HBM)
    dma = pltpu.SemaphoreType.DMA
    dtype = tokens.dtype
    block = columns * tp_size * kv_rows
    rows = tp_size * tokens.shape[0]
    each = q_rows + 2 * kv_rows
    total = columns * tp_size * each
    vmem = pl.BlockSpec(memory_space=pltpu.VMEM)
    inputs = [
        pltpu.with_memory_space_constraint(a, pltpu.HBM)
        for a in (q_weight, key_projection_weight, value_projection_weight, tokens)
    ]
    held = pl.pallas_call(
        functools.partial(gather_kernel, rep_size, tp_size, q_rows, kv_rows, piece, twice),
        out_shape=(
            pltpu.VMEM((total, width), dtype),
            pltpu.VMEM((rows, width), dtype),
            pltpu.VMEM((rows, total), dtype),
        ),
        in_specs=[hbm] * 4,
        out_specs=(vmem,) * 3,
        scratch_shapes=[
            pltpu.VMEM((count * piece, width), dtype),
            pltpu.VMEM((each, width), dtype),
            pltpu.VMEM((each, width), q_weight.dtype),
            dma((3,)), dma((1,)),
            dma((1,)), dma((pieces,)),
            dma((2, 2)), dma((2, count)),
            dma((1,)), dma((count,)),
            dma((columns - 1,)), dma((columns - 1, 4)),
            dma((3,)), dma((3,)),
            dma((columns - 1, max(twice, 1))), dma((2,)), dma((columns - 1, max(twice, 1))),
        ],
        compiler_params=pltpu.CompilerParams(
            has_side_effects=True, collective_id=0, vmem_limit_bytes=VMEM * 2**20
        ),
    )(*inputs)
    blocks = total // block
    return pl.pallas_call(
        functools.partial(finish_kernel, columns, tp_size, q_rows, kv_rows),
        out_shape=(
            jax.ShapeDtypeStruct((total, width), dtype),
            jax.ShapeDtypeStruct((rows, total), dtype),
        ),
        in_specs=[vmem] * 3,
        out_specs=(hbm, hbm),
        scratch_shapes=[
            pltpu.VMEM((rows, total), dtype), dma((blocks,)), dma((blocks,)), dma((blocks,)),
        ],
        compiler_params=pltpu.CompilerParams(vmem_limit_bytes=VMEM * 2**20),
    )(*held)


def solution(mesh):
    spec = P(("rep", "tp"), None)
    return jax.shard_map(
        shards, mesh=mesh, in_specs=(spec,) * 4, out_specs=(P("tp", None), P("rep", "tp")), check_vma=False
    )
```

time: 247 us -> 201 us (0.81); the launches traced: 244 us -> 201 us
  Pallas kernels: 230 us -> 200 us
  local copies, waits for them, and re-layouts: 8.79 us -> 0 us
  other arithmetic: 4.68 us -> 0 us
    pallas_call x1 -> x2, Pallas kernels: 230 us -> 200 us  [the longest x1 192 us: shards(): pl.pallas_call(functools.partial(gather_kernel, rep_size, tp_size, q_rows...]
    unnamed x4 -> x0, local copies, waits for them, and re-layouts: 8.79 us -> none
    another operation x3 -> x0, other arithmetic: 4.53 us -> none
where the time goes in v1:
time: 201 us
  Pallas kernels  200 us (100%)
    pallas_call x1, Pallas kernels, shards(): pl.pallas_call(functools.partial(gather_kernel, rep_size, tp_size, q_rows...  192 us
    pallas_call x1, Pallas kernels, shards(): pl.pallas_call(functools.partial(finish_kernel, columns, tp_size, q_rows,...  8.03 us

profile of v1, /device:TPU:24, one launch (start us, length us, event | category | flops | bytes accessed | tf_op | source)
XLA Modules:
  0.0 201.0 jit_solution(2593891193732591210)
XLA Ops:
  0.6 192.3 %shard_map.59 = (bf16[1792,5120]{1,0:T(8,128)(2,1)S(1)}, bf16[1024,5120]{1,0:T(8,128)(2,1)S(1)}, bf16[1024,1792]{1,0:T(8,128)(2,1)S(1)}) custom-call(f32[160,5120]{1,0:T(8,128)} %q_weight.1, f32[32,5120]{1,0:T(8,128)} %k_weight.1, f32[32,5120]{1,0:T(8,128)} %v_weight.1, bf16[256,5120]{1,0:T(8,128)(2,1)} %tok.1), custom_call_target="tpu_custom_call" | custom-call | tf_op jit(solution)/shard_map/pallas_call | solution.py:537
  192.9 8.0 %shard_map.60 = (bf16[1792,5120]{1,0:T(8,128)(2,1)}, bf16[1024,1792]{1,0:T(8,128)(2,1)}) custom-call(bf16[1792,5120]{1,0:T(8,128)(2,1)S(1)} %get-tuple-element.5.weights, bf16[1024,5120]{1,0:T(8,128)(2,1)S(1)} %get-tuple-element.6.prompts, bf16[1024,1792]{1,0:T(8,128)(2,1)S(1)} %get-tuple-element.7.partial), custom_call_target="tpu_custom_call" | custom-call | tf_op jit(solution)/shard_map/pallas_call | solution.py:563

commit v2 on v1

--- a/solution.py
+++ b/solution.py
@@ -10,7 +10,7 @@
 MESH = pl.DeviceIdType.MESH
 LEAD = 4
 Y_LAG = 3
-LATE_FIRST = (4, 2)
+LATE_FIRST = (1, 2)
 LATE_RATE = (6, 5)
 TOK_FIRST = 2
 TOK_AT = 8
@@ -19,32 +19,24 @@
 TWIN_AT = 18
 TWIN_RATE = 4
 FAR_AT = 24
-MEET_AT = 24
-FIRST_AT = (99, 99)
+MEET_AT = 22
+BLOCK_AT = (6, 12)
 TWICE = (17, 28)
-TILE = 256
-VMEM = 16
-
-
-def order_of(columns, tp_size, q_rows, kv_rows, column, side):
+NEAR = (14, 28)
+CROSS = 1
+TILE = 512
+VMEM = 20
+
+
+def order_of(columns, tp_size, q_rows, kv_rows, column):
     block = columns * tp_size * kv_rows
     own = tp_size * q_rows
     firsts = [-(-(c * own) // block) for c in range(columns)]
     early = max(min((c + 1) * own // block - firsts[c] for c in range(columns)), 0)
     q_blocks = columns * own // block
     first = (column * own + block - 1) // block
-    left = q_blocks - early
-    places = [jnp.where(side == 0, left - 1 - i, i) for i in range(left)]
-    last = [jnp.where(i >= first, i + early, i) for i in places]
-    alone = left > 1
-    for c in range(columns):
-        for s in range(2):
-            i = 0 if s else left - 1
-            low = (i + early if i >= firsts[c] else i) * block
-            for part in range(low // (2 * q_rows), (low + block - 1) // (2 * q_rows) + 1):
-                alone = alone and (part // 2 == c or part % 2 != s)
-    here = [q_blocks, q_blocks + 1] + [first + i for i in range(early)]
-    return here + last, len(here), int(alone)
+    rest = [jnp.where(i >= first, i + early, i) for i in range(q_blocks - early)]
+    return [first + i for i in range(early)] + rest + [q_blocks, q_blocks + 1], early
 
 
 def multiply(index, prompts, weights, result, at, block):
@@ -67,8 +59,8 @@
 ):
     r, t = lax.axis_index("rep"), lax.axis_index("tp")
     block = columns * tp_size * kv_rows
-    blocks, soon, late_block = order_of(columns, tp_size, q_rows, kv_rows, r % columns, t // 2)
-    done = soon + late_block
+    blocks, _ = order_of(columns, tp_size, q_rows, kv_rows, r % columns)
+    done = len(blocks) - 2
     stores = []
     for i in range(weights.shape[0] // block):
         at = pl.ds(i * block, block)
@@ -89,11 +81,11 @@
 
 
 def gather_kernel(
-    rep_size, tp_size, q_rows, kv_rows, piece, twice,
+    rep_size, tp_size, q_rows, kv_rows, piece, twice, near,
     q_weight, k_weight, v_weight, tok, weights, prompts, projected,
     relay, shard, wide, load_sem, local_sem,
     part_send, part_recv, z_send, z_recv, y_send, y_recv, x_send, x_recv, tok_send, tok_recv,
-    pair_recv, twin_send, twin_recv,
+    pair_recv, twin_send, twin_recv, cross_send, cross_recv,
 ):
     planes = tp_size
     columns = rep_size // planes
@@ -107,24 +99,22 @@
     q_pieces = q_rows // piece
     pieces = q_pieces + 2 * split
     count = 2 * pieces
-    small = 4 * split
+    large = 2 * q_pieces
     shards_in_plane = tp_size * columns
     ranks = (t, other)
-    sequence = [(True, m) for m in range(2 * split)] + [(False, m) for m in range(2 * split)]
-    for m in range(2 * split, pieces):
-        sequence += [(True, m), (False, m)]
-
-    def shard_row(m):
-        return q_rows + m * piece if m < 2 * split else (m - 2 * split) * piece
+
+    def sequence(n):
+        return n % 2 == 0, n // 2
 
     def row_of(index, m):
-        if m >= 2 * split:
-            return pl.multiple_of(index * q_rows + (m - 2 * split) * piece, 8)
+        if m < q_pieces:
+            return pl.multiple_of(index * q_rows + m * piece, 8)
+        m -= q_pieces
         base = shards_in_plane * (q_rows + (m // split) * kv_rows) + (m % split) * piece
         return pl.multiple_of(base + index * kv_rows, 8)
 
     def in_weights(at_column, at_side, n):
-        own, m = sequence[n]
+        own, m = sequence(n)
         of_core = core if own else 1 - core
         return weights.at[pl.ds(row_of(at_column * tp_size + at_side * 2 + of_core, m), piece)]
 
@@ -132,7 +122,7 @@
         return relay.at[pl.ds(n * piece, piece)]
 
     def in_shard(m):
-        return shard.at[pl.ds(shard_row(m), piece)]
+        return shard.at[pl.ds(m * piece, piece)]
 
     def place(slot, n):
         return in_weights(column, side, n) if slot == 0 else in_relay(n)
@@ -151,6 +141,14 @@
 
     def reached(k, at):
         return (at != k) & (inner(k) | (at == k + 1) | (at == k - 1))
+
+    def beside(k, at):
+        return ((k == 1) & (at == 0)) | ((k == planes - 2) & (at == planes - 1))
+
+    def doubled(n, at):
+        if n >= count - near:
+            return reached(t, at)
+        return reached(t, at) & jnp.logical_not(beside(t, at))
 
     def is_twice(n):
         return n >= count - twice
@@ -190,13 +188,13 @@
         if slot == 1:
             remote(src, in_weights(column, side, n), y_send.at[0], y_recv.at[n], r, other).start()
         elif not is_twice(n):
-            x_sends(n, src, dst, lambda d: x_recv.at[d, 0 if n < small else 1])
+            x_sends(n, src, dst, lambda d: x_recv.at[d, 1 if n < large else 0])
         elif source:
             x_sends(n, src, dst, lambda d: pair_recv.at[d, n - (count - twice)])
         else:
-            @pl.when(jnp.logical_not(reached(t, plane)))
+            @pl.when(jnp.logical_not(doubled(n, plane)))
             def _():
-                x_sends(n, src, dst, lambda d: x_recv.at[d, 3])
+                x_sends(n, src, dst, lambda d: x_recv.at[d, 3 if n < large else 4])
 
     def span(n):
         return weights.at[pl.ds(0, n * piece)]
@@ -208,14 +206,14 @@
         remote(src, src, sem, x_recv.at[0, 0], r, partner).wait_send()
 
     def at_source(slot, n):
-        own, m = sequence[n]
+        own, m = sequence(n)
         return in_shard(m) if own else place(slot, n)
 
     taken = [0, 0]
 
     def take(slot, n):
         while taken[slot] <= n:
-            own, m = sequence[taken[slot]]
+            own, m = sequence(taken[slot])
             if not own:
                 @pl.when(plane == ranks[slot])
                 def _():
@@ -231,6 +229,8 @@
 
     def late_step(slot, n):
         take(slot, n)
+        if slot == 1 and n < CROSS:
+            return
         late_up, late_down = held_back(slot)
         src, dst = at_source(slot, n), place(slot, n)
 
@@ -244,6 +244,8 @@
 
     def relay_step(slot, n, late):
         sink = late_sink(slot)
+        if slot == 1 and late and n < CROSS:
+            return
 
         @pl.when((plane != ranks[slot]) & (sink if late else jnp.logical_not(sink)))
         def _():
@@ -256,32 +258,45 @@
         @pl.when(sink if late else jnp.logical_not(sink))
         def _():
             block = in_weights(column, 1 - side, n)
-            recv_wait(block, y_recv.at[n])
-            x_sends(n, block, block, lambda d: x_recv.at[d, 0 if n < small else 2])
-
-    goes_up = (plane >= t) & (plane < planes - 1) & reached(t, plane + 1)
-    goes_down = (plane <= t) & (plane > 0) & reached(t, plane - 1)
-    goes = goes_up | goes_down
+            recv_wait(block, cross_recv.at[n] if late and n < CROSS else y_recv.at[n])
+            x_sends(n, block, block, lambda d: x_recv.at[d, 2 if n < large else 0])
+            if n < CROSS and not late:
+                @pl.when((plane == t) & (t == 1))
+                def _():
+                    remote(block, block, cross_send.at[0], cross_recv.at[n], r - columns, t).start()
+
+                @pl.when((plane == t) & (t == planes - 2))
+                def _():
+                    remote(block, block, cross_send.at[0], cross_recv.at[n], r + columns, t).start()
+
+    def goes_up(n):
+        return (plane >= t) & (plane < planes - 1) & doubled(n, plane + 1)
+
+    def goes_down(n):
+        return (plane <= t) & (plane > 0) & doubled(n, plane - 1)
+
+    def goes(n):
+        return goes_up(n) | goes_down(n)
 
     def twin_step(d, n, source):
         src = twin_place(d, n)
         at = n - (count - twice)
-        here = plane == t if source else (plane != t) & goes
+        here = plane == t if source else (plane != t) & goes(n)
 
         @pl.when(here)
         def _():
             recv_wait(src, pair_recv.at[d - 1, at] if source else twin_recv.at[d - 1, at])
 
-        @pl.when(here & goes_up)
+        @pl.when(here & goes_up(n))
         def _():
             remote(src, src, twin_send.at[0], twin_recv.at[d - 1, at], r + columns, t).start()
 
-        @pl.when(here & goes_down)
+        @pl.when(here & goes_down(n))
         def _():
             remote(src, src, twin_send.at[1], twin_recv.at[d - 1, at], r - columns, t).start()
 
     def twin_sink(d, n):
-        @pl.when(reached(t, plane) & jnp.logical_not(goes))
+        @pl.when(doubled(n, plane) & jnp.logical_not(goes(n)))
         def _():
             recv_wait(twin_place(d, n), twin_recv.at[d - 1, n - (count - twice)])
 
@@ -313,10 +328,15 @@
     greet(r, other)
     greet(r, partner)
 
+    chunks = q_rows // kv_rows
     loads = [
-        pltpu.make_async_copy(k_weight, wide.at[pl.ds(q_rows, kv_rows)], load_sem.at[0]),
-        pltpu.make_async_copy(v_weight, wide.at[pl.ds(q_rows + kv_rows, kv_rows)], load_sem.at[1]),
-        pltpu.make_async_copy(q_weight, wide.at[pl.ds(0, q_rows)], load_sem.at[2]),
+        pltpu.make_async_copy(
+            q_weight.at[pl.ds(i * kv_rows, kv_rows)], wide.at[pl.ds(i * kv_rows, kv_rows)], load_sem.at[i]
+        )
+        for i in range(chunks)
+    ] + [
+        pltpu.make_async_copy(w, wide.at[pl.ds(q_rows + i * kv_rows, kv_rows)], load_sem.at[chunks + i])
+        for i, w in enumerate((k_weight, v_weight))
     ]
     load_tok = pltpu.make_async_copy(tok, prompt_rows(t), local_sem.at[0])
     for load in loads:
@@ -324,7 +344,7 @@
     load_tok.start()
 
     def cast(m):
-        at = pl.ds(shard_row(m), piece)
+        at = pl.ds(m * piece, piece)
         value = wide[at, :].astype(shard.dtype)
         shard[at, :] = value
 
@@ -342,25 +362,24 @@
 
             @pl.when(side != plane // 2)
             def _():
-                remote(in_shard(m), in_relay(sequence.index((False, m))), part_send.at[0], part_recv.at[m], r, partner).start()
+                remote(in_shard(m), in_relay(2 * m + 1), part_send.at[0], part_recv.at[m], r, partner).start()
 
     loads[0].wait()
-    loads[1].wait()
-    for m in range(2 * split):
+    for m in range(split):
         cast(m)
     neighbours = columns + 1 + jnp.where(inner(plane), 2, 1)
     pl.semaphore_wait(barrier, neighbours)
-    for m in range(2 * split):
+    for m in range(split):
         part(m)
     lead = min(LEAD, 2 * split)
     for n in range(lead):
         source_step(0, n)
         source_step(1, n)
-    loads[2].wait()
-    for m in range(2 * split, pieces):
-        cast(m)
-    for m in range(2 * split, pieces):
-        part(m)
+    for i in range(1, chunks + 2):
+        loads[i].wait()
+        for m in range(i * split, (i + 1) * split):
+            cast(m)
+            part(m)
     for n in range(lead, LEAD):
         source_step(0, n)
         source_step(1, n)
@@ -370,7 +389,7 @@
     late, sunk, late_y, sent, twins, far = [0, 0], [0, 0], 0, 0, 0, 0
     pairs = [(d, n) for n in range(count - twice, count) for d in range(1, columns)]
     block = shards_in_plane * kv_rows
-    blocks, soon, late_block = order_of(columns, tp_size, q_rows, kv_rows, column, side)
+    blocks, own_blocks = order_of(columns, tp_size, q_rows, kv_rows, column)
 
     def late_to(slot, stop):
         while late[slot] < min(stop, count):
@@ -414,8 +433,29 @@
     def begin():
         recv_wait(prompt_rows(partner), tok_recv.at[1])
         recv_wait(prompt_rows((partner + half) % tp_size), tok_recv.at[2])
+
+    def arrive(first, stop, sems):
+        plain = max(min(stop, count - twice) - first, 0)
+        extra = stop - first - plain
         for d in range(1, columns):
-            recv_wait(span(2 * small), x_recv.at[d - 1, 0])
+            if sems[0] != sems[1]:
+                if plain:
+                    recv_wait(span(plain), x_recv.at[d - 1, sems[0]])
+                recv_wait(span(stop - first), x_recv.at[d - 1, sems[1]])
+            else:
+                recv_wait(span(plain + stop - first), x_recv.at[d - 1, sems[0]])
+            if extra:
+                @pl.when((plane != t) & jnp.logical_not(reached(t, plane)))
+                def _():
+                    recv_wait(span(extra), x_recv.at[d - 1, sems[2]])
+            single = max(min(stop, count - near) - max(first, count - twice), 0)
+            if single:
+                @pl.when(beside(t, plane))
+                def _():
+                    recv_wait(span(single), x_recv.at[d - 1, sems[2]])
+        for d, n in pairs:
+            if first <= n < stop:
+                twin_sink(d, n)
 
     send_tokens(TOK_FIRST)
     for slot in range(2):
@@ -441,69 +481,55 @@
             far_to((n - FAR_AT) * TWIN_RATE // 4 + 1)
         if n == MEET_AT:
             meet()
-        for i in range(2):
-            if n == FIRST_AT[i]:
-                if i == 0:
-                    begin()
-                multiply(blocks[i], prompts, weights, projected, None, block)
     for slot in range(2):
         late_to(slot, count)
     for n in range(count - Y_LAG, count):
         y_step(n, False)
-    early = [i for i in range(2) if FIRST_AT[i] < count]
     if MEET_AT >= count:
         meet()
-    if not early:
-        begin()
-    rest = [i for i in range(soon) if i not in early]
+    begin()
     twins_to(len(pairs))
-    before = [i for i in rest if i < 2]
-    after = [i for i in rest if i >= 2]
-    steps = max(count - min(sunk), 1)
-    for k in range(steps):
-        for slot in range(2):
-            sink_to(slot, max(sunk[slot], min(sunk) + 1) if k < steps - 1 else count)
-        late_y_to(min(sunk) - Y_LAG)
-        far_to(len(pairs) * (k + 1) // steps)
-        if before and (k + 1) % max(steps // (len(before) + 1), 1) == 0:
-            multiply(blocks[before.pop(0)], prompts, weights, projected, None, block)
+    done = 0
+
+    def multiply_to(stop):
+        nonlocal done
+        while done < stop:
+            if done == own_blocks:
+                arrive(0, large, (1, 2, 3))
+            multiply(blocks[done], prompts, weights, projected, None, block)
+            done += 1
+
+    for slot in range(2):
+        sink_to(slot, count)
     late_y_to(count)
-    far_to(len(pairs))
-    for i in before + after:
-        multiply(blocks[i], prompts, weights, projected, None, block)
-    for d in range(1, columns):
-        recv_wait(span(count - small), x_recv.at[d - 1, 2])
-    if late_block:
-        multiply(blocks[soon], prompts, weights, projected, None, block)
-    for d, n in pairs:
-        twin_sink(d, n)
-    for d in range(1, columns):
-        recv_wait(span(count - twice - small), x_recv.at[d - 1, 1])
-        if twice:
-            @pl.when((plane != t) & jnp.logical_not(reached(t, plane)))
+    for i in range(len(pairs)):
+        far_to(i + 1)
+        multiply_to(sum(i >= at for at in BLOCK_AT[:own_blocks]))
+    multiply_to(len(blocks) - 2)
+    arrive(large, count, (0, 0, 4))
+
+    def sent_when(go, n, sem):
+        if n:
+            @pl.when(go)
             def _():
-                recv_wait(span(twice), x_recv.at[d - 1, 3])
+                send_wait(span(n), sem)
 
     for d in range(1, columns):
         send_wait(span(2 * count - twice), x_send.at[d - 1])
-        if twice:
-            @pl.when(jnp.logical_not(reached(t, plane)))
-            def _():
-                send_wait(span(twice), x_send.at[d - 1])
-    send_wait(relay, y_send.at[0])
+        sent_when(jnp.logical_not(reached(t, plane)), twice, x_send.at[d - 1])
+        sent_when(beside(t, plane), twice - near, x_send.at[d - 1])
+    send_wait(span(count - CROSS), y_send.at[0])
+    sent_when(jnp.logical_not(late_sink(1)), CROSS, y_send.at[0])
     for slot in range(2):
-        for way, go in enumerate(ups(slot)):
-            @pl.when(go)
-            def _():
-                send_wait(relay, z_send.at[slot, way])
+        for way in range(2):
+            go, held = ups(slot)[way], held_back(slot)[way]
+            sent_when(go, count - CROSS, z_send.at[slot, way])
+            sent_when(go & jnp.logical_not(held) if slot else go, CROSS, z_send.at[slot, way])
     if twice:
-        @pl.when(goes_up)
-        def _():
-            send_wait(span(twice * (columns - 1)), twin_send.at[0])
-
-        @pl.when(goes_down)
-        def _():
-            send_wait(span(twice * (columns - 1)), twin_send.at[1])
+        for way, go in enumerate((goes_up, goes_down)):
+            sent_when(go(count - 1), near * (columns - 1), twin_send.at[way])
+            sent_when(go(count - twice), (twice - near) * (columns - 1), twin_send.at[way])
+    sent_when((plane == t) & inner(t), CROSS, cross_send.at[0])
 
     @pl.when(jnp.logical_not(handler))
     def _():
@@ -521,7 +547,7 @@
     piece = kv_rows // 2 if kv_rows % 32 == 0 else kv_rows
     pieces = (q_rows + 2 * kv_rows) // piece
     count = 2 * pieces
-    twice = count * TWICE[0] // TWICE[1] if columns == 2 else 0
+    twice, near = [count * a // b if columns == 2 else 0 for a, b in (TWICE, NEAR)]
     hbm = pl.BlockSpec(memory_space=pltpu.HBM)
     dma = pltpu.SemaphoreType.DMA
     dtype = tokens.dtype
@@ -535,7 +561,7 @@
         for a in (q_weight, key_projection_weight, value_projection_weight, tokens)
     ]
     held = pl.pallas_call(
-        functools.partial(gather_kernel, rep_size, tp_size, q_rows, kv_rows, piece, twice),
+        functools.partial(gather_kernel, rep_size, tp_size, q_rows, kv_rows, piece, twice, near),
         out_shape=(
             pltpu.VMEM((total, width), dtype),
             pltpu.VMEM((rows, width), dtype),
@@ -547,13 +573,14 @@
             pltpu.VMEM((count * piece, width), dtype),
             pltpu.VMEM((each, width), dtype),
             pltpu.VMEM((each, width), q_weight.dtype),
-            dma((3,)), dma((1,)),
+            dma((q_rows // kv_rows + 2,)), dma((1,)),
             dma((1,)), dma((pieces,)),
             dma((2, 2)), dma((2, count)),
             dma((1,)), dma((count,)),
-            dma((columns - 1,)), dma((columns - 1, 4)),
+            dma((columns - 1,)), dma((columns - 1, 5)),
             dma((3,)), dma((3,)),
             dma((columns - 1, max(twice, 1))), dma((2,)), dma((columns - 1, max(twice, 1))),
+            dma((1,)), dma((max(CROSS, 1),)),
         ],
         compiler_params=pltpu.CompilerParams(
             has_side_effects=True, collective_id=0, vmem_limit_bytes=VMEM * 2**20
@@ -569,7 +596,7 @@
         in_specs=[vmem] * 3,
         out_specs=(hbm, hbm),
         scratch_shapes=[
-            pltpu.VMEM((rows, total), dtype), dma((blocks,)), dma((blocks,)), dma((blocks,)),
+            pltpu.VMEM((rows, 2 * block), dtype), dma((blocks,)), dma((blocks,)), dma((2,)),
         ],
         compiler_params=pltpu.CompilerParams(vmem_limit_bytes=VMEM * 2**20),
     )(*held)

time: 201 us -> 196 us (0.975)
  Pallas kernels: 200 us -> 195 us
    pallas_call x1, Pallas kernels: 192 us -> 187 us  [shards(): pl.pallas_call(functools.partial(gather_kernel, rep_size, tp_size, q_rows...]
where the time goes in v2:
time: 196 us; the launch traced here: 195 us
  Pallas kernels  195 us (99%)
    pallas_call x1, Pallas kernels, shards(): pl.pallas_call(functools.partial(gather_kernel, rep_size, tp_size, q_rows...  187 us
    pallas_call x1, Pallas kernels, shards(): pl.pallas_call(functools.partial(finish_kernel, columns, tp_size, q_rows,...  7.55 us

profile of v2, /device:TPU:24, one launch (start us, length us, event | category | flops | bytes accessed | tf_op | source)
XLA Modules:
  0.0 195.4 jit_solution(16362553151298233956)
XLA Ops:
  0.6 187.0 %shard_map.59 = (bf16[1792,5120]{1,0:T(8,128)(2,1)S(1)}, bf16[1024,5120]{1,0:T(8,128)(2,1)S(1)}, bf16[1024,1792]{1,0:T(8,128)(2,1)S(1)}) custom-call(f32[160,5120]{1,0:T(8,128)} %q_weight.1, f32[32,5120]{1,0:T(8,128)} %k_weight.1, f32[32,5120]{1,0:T(8,128)} %v_weight.1, bf16[256,5120]{1,0:T(8,128)(2,1)} %tok.1), custom_call_target="tpu_custom_call" | custom-call | tf_op jit(solution)/shard_map/pallas_call | solution.py:563
  187.7 7.5 %shard_map.60 = (bf16[1792,5120]{1,0:T(8,128)(2,1)}, bf16[1024,1792]{1,0:T(8,128)(2,1)}) custom-call(bf16[1792,5120]{1,0:T(8,128)(2,1)S(1)} %get-tuple-element.5.weights, bf16[1024,5120]{1,0:T(8,128)(2,1)S(1)} %get-tuple-element.6.prompts, bf16[1024,1792]{1,0:T(8,128)(2,1)S(1)} %get-tuple-element.7.partial), custom_call_target="tpu_custom_call" | custom-call | tf_op jit(solution)/shard_map/pallas_call | solution.py:590

commit v3 on v2

--- a/solution.py
+++ b/solution.py
@@ -427,6 +427,7 @@
             far += 1
 
     def meet():
+        send_tokens(TOK_CHUNKS)
         recv_wait(prompt_rows(other), tok_recv.at[0])
         remote(prompt_rows(other), prompt_rows(other), tok_send.at[2], tok_recv.at[2], r, partner).start()
 

time: 196 us -> 196 us (level)
  no operation moved by 1% of the time
where the time goes in v3:
time: 196 us; the launch traced here: 195 us
  Pallas kernels  195 us (99%)
    pallas_call x1, Pallas kernels, shards(): pl.pallas_call(functools.partial(gather_kernel, rep_size, tp_size, q_rows...  187 us
    pallas_call x1, Pallas kernels, shards(): pl.pallas_call(functools.partial(finish_kernel, columns, tp_size, q_rows,...  7.55 us

profile of v3, /device:TPU:24, one launch (start us, length us, event | category | flops | bytes accessed | tf_op | source)
XLA Modules:
  0.0 195.4 jit_solution(16362553151298233956)
XLA Ops:
  0.6 187.0 %shard_map.59 = (bf16[1792,5120]{1,0:T(8,128)(2,1)S(1)}, bf16[1024,5120]{1,0:T(8,128)(2,1)S(1)}, bf16[1024,1792]{1,0:T(8,128)(2,1)S(1)}) custom-call(f32[160,5120]{1,0:T(8,128)} %q_weight.1, f32[32,5120]{1,0:T(8,128)} %k_weight.1, f32[32,5120]{1,0:T(8,128)} %v_weight.1, bf16[256,5120]{1,0:T(8,128)(2,1)} %tok.1), custom_call_target="tpu_custom_call" | custom-call | tf_op jit(solution)/shard_map/pallas_call | solution.py:564
  187.7 7.5 %shard_map.60 = (bf16[1792,5120]{1,0:T(8,128)(2,1)}, bf16[1024,1792]{1,0:T(8,128)(2,1)}) custom-call(bf16[1792,5120]{1,0:T(8,128)(2,1)S(1)} %get-tuple-element.5.weights, bf16[1024,5120]{1,0:T(8,128)(2,1)S(1)} %get-tuple-element.6.prompts, bf16[1024,1792]{1,0:T(8,128)(2,1)S(1)} %get-tuple-element.7.partial), custom_call_target="tpu_custom_call" | custom-call | tf_op jit(solution)/shard_map/pallas_call | solution.py:591
